TPU v7x, 32 devices: a 4x4x1 block of a 4x4x8 slice. The times are simulated.
32 devices in a mesh: dp: 2 (over z, core), tp: 16 (over x, y).
Axes of the slice: x: 4, y: 4, z: 1, core: 2. Of those that a mesh axis runs over, the one named last changes fastest.
The devices are a block of a 4x4x8 slice.
Arguments:
- x: bfloat16 [256, 8192], P('dp'), parts along dimension 0
- w_gate: bfloat16 [8192, 24576], P(None, 'tp')
- w_up: bfloat16 [8192, 24576], P(None, 'tp')
- w_down: bfloat16 [24576, 8192], P('tp')
Outputs:
- output: bfloat16 [256, 8192], P('dp'), parts along dimension 0
There are 2 independent parts. A program takes and returns all parts, laid end to end along the dimension named above; an argument that names none is the same for every part.
All inputs are finite; a program needn't handle non-finite values.
Results may differ from a plain program's by a relative error of at most 0.016.
Values are sent between devices in bfloat16 or wider.
A program may use at most 768 MiB of HBM per device.

v0:
```python
import jax
import jax.numpy as jnp
from jax import lax
from jax.sharding import PartitionSpec as P


def solution(mesh):
    def step(x, w_gate, w_up, w_down):
        gate = jnp.dot(x, w_gate, preferred_element_type=jnp.float32)
        up = jnp.dot(x, w_up, preferred_element_type=jnp.float32)
        hidden = (jax.nn.silu(gate) * up).astype(jnp.bfloat16)
        term = jnp.dot(hidden, w_down, preferred_element_type=jnp.float32).astype(jnp.bfloat16)
        return lax.psum(term, "tp")

    return jax.shard_map(
        step,
        mesh=mesh,
        in_specs=(P("dp", None), P(None, "tp"), P(None, "tp"), P("tp", None)),
        out_specs=P("dp", None),
        check_vma=False,
    )
```

profile of v0, /device:TPU:96, one launch (start us, length us, event | category | flops | bytes accessed | tf_op | source)
XLA Modules:
  0.0 130.9 jit_solution(11467931092954491101)
XLA Ops:
  6.5 0.0 copy-start
  6.6 0.0 all-reduce.2.cloned.1.call-start
  6.6 1.6 %copy-done = bf16[128,8192]{1,0:T(8,128)(2,1)S(1)} copy-done((bf16[128,8192]{1,0:T(8,128)(2,1)S(1)}, bf16[128,8192]{1,0:T(8,128)(2,1)}, u32[]{:S(2)}) %copy-start) | copy-done | bytes 2097176
  8.1 10.0 %fusion.8 = f32[128,1536]{1,0:T(8,128)S(1)} fusion(bf16[128,8192]{1,0:T(8,128)(2,1)S(1)} %copy-done, bf16[8192,1536]{1,0:T(8,128)(2,1)} %param.5), kind=kOutput, calls=%fused_computation.10 | convolution fusion | flops 3221225472 | bytes 28049408 | tf_op jit(solution)/shard_map/dot_general | solution.py:9
  18.1 19.7 %convolution_convert_fusion = bf16[128,8192]{1,0:T(8,128)(2,1)} fusion(bf16[1536,8192]{1,0:T(8,128)(2,1)} %param.7, bf16[128,8192]{1,0:T(8,128)(2,1)S(1)} %copy-done, bf16[8192,1536]{1,0:T(8,128)(2,1)} %param.6, f32[128,1536]{1,0:T(8,128)S(1)} %fusion.8), kind=kOutput, calls=%fused_computation | convolution fusion | flops 6444679168 | bytes 55312384 | tf_op jit(solution)/shard_map/dot_general | solution.py:12
  37.8 0.1 all-reduce.2.cloned.1.call-update
  37.9 83.1 %all-reduce.2.cloned.1.call-done = bf16[128,8192]{1,0:T(8,128)(2,1)} async-done(((bf16[128,8192]{1,0:T(8,128)(2,1)}), bf16[128,8192]{1,0:T(8,128)(2,1)}) %all-reduce.2.cloned.1.call-update) | async-done | bytes 2097168 | tf_op jit(solution)/shard_map/psum | solution.py:13
  121.0 3.1 %copy.6 = bf16[128,8192]{1,0:T(8,128)(2,1)} copy(bf16[128,8192]{1,0:T(8,128)(2,1)} %all-reduce.2.cloned.1.call-done) | data formatting | bytes 4194304
Async XLA Ops:
  6.5 1.6 %copy-start = (bf16[128,8192]{1,0:T(8,128)(2,1)S(1)}, bf16[128,8192]{1,0:T(8,128)(2,1)}, u32[]{:S(2)}) copy-start(bf16[128,8192]{1,0:T(8,128)(2,1)} %param.4) | copy-start | bytes 6291460
  6.6 114.4 %all-reduce.2.cloned.1.call-start = ((), (), s32[]{:S(2)}) async-start(), calls=%async_computation | async-start | bytes 4194304 | tf_op jit(solution)/shard_map/psum | solution.py:13
Sparse Core Ops, SparseCore 0:
  38.0 82.9 all-reduce.1
where the time goes:
time: 131 us
  waiting for transfers between devices  83.1 us (63%)
  matrix products  29.7 us (23%)
  between operations  13.4 us (10%)
  local copies, waits for them, and re-layouts  4.68 us (4%)
    psum x1, waiting for transfers between devices, step(): return lax.psum(term, 'tp')  83.1 us
    dot_general x1, matrix products, step(): jnp.dot(hidden, w_down, preferred_element_type=jnp.float32)  19.7 us
    dot_general x1, matrix products, step(): gate = jnp.dot(x, w_gate, preferred_element_type=jnp.float32)  9.98 us
    unnamed x3, local copies, waits for them, and re-layouts  4.68 us
  transfers between devices with their start and end apart: 1, of which 1 were waited for; matrix products, arithmetic and copies ran while one was open for 0% of the time, Pallas kernels for 0%

commit v1 on v0

v1 whole, which is shorter than its diff:
```python
import functools

import jax
import jax.numpy as jnp
from jax import lax
from jax.experimental import pallas as pl
from jax.experimental.pallas import tpu as pltpu
from jax.sharding import PartitionSpec as P

MESH = pl.DeviceIdType.MESH
CHUNKS = 2
NBLOCK = 512
KCHUNK = 1024
DEPTH = 4
AHEAD = 4
BF16, F32 = jnp.bfloat16, jnp.float32


def kernel(
    chunks, kchunk, nblock, depth,
    x_hbm, wg_hbm, wu_hbm, wd_hbm, y,
    xv, gb, ub, wdb, accg, accu, hid,
    own, keep, sstep, sdir, smrg, rstep, rdir, rmrg,
    tstep, tdir, tmrg, qstep, qdir, qmrg,
    xsem, gsem, usem, wsem, ssem, rsem,
):
    n = lax.axis_size("tp")
    side = 4
    me = lax.axis_index("tp")
    px, py = me // side, lax.rem(me, side)

    def at(i, j):
        return lax.rem(i + side, side) * side + lax.rem(j + side, side)

    axes = (
        ((px, at(px + 1, py), at(px - 1, py)), (py, at(px, py + 1), at(px, py - 1))),
        ((py, at(px, py + 1), at(px, py - 1)), (px, at(px + 1, py), at(px - 1, py))),
    )

    barrier = pltpu.get_barrier_semaphore()
    for _, plus, minus in axes[0]:
        for dev in (plus, minus):
            pl.semaphore_signal(barrier, inc=1, device_id={"tp": dev}, device_id_type=MESH)

    rows = xv.shape[1]
    ksteps = wg_hbm.shape[0] // kchunk
    nblocks = wg_hbm.shape[1] // nblock
    steps = ksteps * nblocks
    width = y.shape[1] // (2 * chunks * side)
    half, quarter, eighth = rows // 2, rows // 4, rows // 8

    def xcopy(k):
        return pltpu.make_async_copy(x_hbm.at[:, pl.ds(k * kchunk, kchunk)], xv.at[k], xsem.at[k])

    def gcopy(i, slot):
        nb, k = i // ksteps, lax.rem(i, ksteps)
        src = (pl.ds(k * kchunk, kchunk), pl.ds(nb * nblock, nblock))
        return (
            pltpu.make_async_copy(wg_hbm.at[src], gb.at[slot], gsem.at[slot]),
            pltpu.make_async_copy(wu_hbm.at[src], ub.at[slot], usem.at[slot]),
        )

    def cols(h, c, seg):
        return pl.ds(pl.multiple_of(((h * chunks + c) * side + seg) * width, width), width)

    order = []
    for c in range(chunks):
        for off in (2, 1, 3, 0):
            for h in range(2):
                order.append((h, c, off))

    def wcopy(j):
        h, c, off = order[j]
        seg = lax.rem(axes[h][0][0] + off, side)
        return pltpu.make_async_copy(wd_hbm.at[:, cols(h, c, seg)], wdb.at[j], wsem.at[j])

    for i in range(depth):
        xcopy(i).start()
        for cp in gcopy(jnp.int32(i), i):
            cp.start()
    for k in range(depth, ksteps):
        xcopy(k).start()

    for nb in range(nblocks):
        accg[...] = jnp.zeros_like(accg)
        accu[...] = jnp.zeros_like(accu)

        @pl.loop(0, ksteps)
        def _(k, nb=nb):
            i = nb * ksteps + k
            slot = lax.rem(i, depth)
            if nb == 0:
                xcopy(k).wait()
            for cp in gcopy(i, slot):
                cp.wait()
            accg[...] += jnp.dot(xv[k], gb[slot], preferred_element_type=F32)
            accu[...] += jnp.dot(xv[k], ub[slot], preferred_element_type=F32)

            @pl.when(i + depth < steps)
            def _():
                for cp in gcopy(i + depth, slot):
                    cp.start()

            if nb == nblocks - 1:
                for d in range(depth):

                    @pl.when(i + depth == steps + d)
                    def _(d=d):
                        if d < len(order):
                            wcopy(d).start()

        g = accg[...]
        hid[:, nb * nblock : (nb + 1) * nblock] = (jax.nn.silu(g) * accu[...]).astype(BF16)

    copies = {}

    def send(h, c, key, slot, src, dst, dev):
        cp = pltpu.make_async_remote_copy(
            src_ref=src, dst_ref=dst, send_sem=ssem.at[h, c, slot], recv_sem=rsem.at[h, c, slot],
            device_id={"tp": dev}, device_id_type=MESH,
        )
        cp.start()
        copies[h, c, key] = cp

    def term(j):
        if j + depth < len(order):
            wcopy(j + depth).start()
        wcopy(j).wait()
        return jnp.dot(hid[...], wdb[j], preferred_element_type=F32)

    def compute(j):
        h, c, off = order[j]
        _, plus, minus = axes[h][0]
        t = term(j)
        if off == 2:
            sstep[h, c] = t.astype(BF16)
            send(h, c, "step+", 0, sstep.at[h, c, :half], rstep.at[h, c, 0], plus)
            send(h, c, "step-", 1, sstep.at[h, c, half:], rstep.at[h, c, 1], minus)
        elif off == 1:
            keep[h, c, 0] = t[:half]
            sdir[h, c, 0] = t[half:].astype(BF16)
            send(h, c, "dir+", 2, sdir.at[h, c, 0], rdir.at[h, c, 0], plus)
        elif off == 3:
            keep[h, c, 1] = t[half:]
            sdir[h, c, 1] = t[:half].astype(BF16)
            send(h, c, "dir-", 3, sdir.at[h, c, 1], rdir.at[h, c, 1], minus)
        else:
            own[h, c] = t

    def merge(h, c):
        _, plus, minus = axes[h][0]
        for d, dev in enumerate((plus, minus)):
            copies[h, c, "step" + "+-"[d]].wait_recv()
            smrg[h, c, d] = (keep[h, c, d] + rstep[h, c, d].astype(F32)).astype(BF16)
            send(h, c, "mrg" + "+-"[d], 4 + d, smrg.at[h, c, d], rmrg.at[h, c, d], dev)

    def sub(p, off, first=0):
        return pl.multiple_of(lax.rem(p + off, side) * quarter + first, eighth)

    def second(h, c):
        for key in ("dir+", "dir-", "mrg+", "mrg-"):
            copies[h, c, key].wait_recv()
        own[h, c, :half] = own[h, c, :half] + (rmrg[h, c, 0].astype(F32) + rdir[h, c, 1].astype(F32))
        own[h, c, half:] = own[h, c, half:] + (rmrg[h, c, 1].astype(F32) + rdir[h, c, 0].astype(F32))
        p, plus, minus = axes[h][1]
        tstep[h, c] = own[h, c, pl.ds(sub(p, 2), quarter)].astype(BF16)
        tdir[h, c, 0] = own[h, c, pl.ds(sub(p, 1, eighth), eighth)].astype(BF16)
        tdir[h, c, 1] = own[h, c, pl.ds(sub(p, 3), eighth)].astype(BF16)
        send(h, c, "step2+", 6, tstep.at[h, c, :eighth], qstep.at[h, c, 0], plus)
        send(h, c, "step2-", 7, tstep.at[h, c, eighth:], qstep.at[h, c, 1], minus)
        send(h, c, "dir2+", 8, tdir.at[h, c, 0], qdir.at[h, c, 0], plus)
        send(h, c, "dir2-", 9, tdir.at[h, c, 1], qdir.at[h, c, 1], minus)

    def merge2(h, c):
        p, plus, minus = axes[h][1]
        for d, dev in enumerate((plus, minus)):
            copies[h, c, "step2" + "+-"[d]].wait_recv()
            mine = own[h, c, pl.ds(sub(p, 1 + 2 * d, eighth * d), eighth)]
            tmrg[h, c, d] = (mine + qstep[h, c, d].astype(F32)).astype(BF16)
            send(h, c, "mrg2" + "+-"[d], 10 + d, tmrg.at[h, c, d], qmrg.at[h, c, d], dev)

    def gather(h, c):
        for key in ("dir2+", "dir2-", "mrg2+", "mrg2-"):
            copies[h, c, key].wait_recv()
        p, plus, minus = axes[h][1]
        pf = axes[h][0][0]
        top = own[h, c, pl.ds(sub(p, 0), eighth)]
        low = own[h, c, pl.ds(sub(p, 0, eighth), eighth)]
        top += qmrg[h, c, 0].astype(F32) + qdir[h, c, 1].astype(F32)
        low += qmrg[h, c, 1].astype(F32) + qdir[h, c, 0].astype(F32)
        y[pl.ds(sub(p, 0), eighth), cols(h, c, pf)] = top.astype(BF16)
        y[pl.ds(sub(p, 0, eighth), eighth), cols(h, c, pf)] = low.astype(BF16)
        mine = y.at[pl.ds(sub(p, 0), quarter), cols(h, c, pf)]
        send(h, c, "ag+", 12, mine, mine, plus)
        send(h, c, "ag-", 13, mine, mine, minus)

    def relay(h, c):
        p, plus, minus = axes[h][1]
        pf = axes[h][0][0]
        for d, dev in enumerate((plus, minus)):
            copies[h, c, "ag" + "+-"[d]].wait_recv()
            piece = y.at[pl.ds(sub(p, 3 - 2 * d, eighth * d), eighth), cols(h, c, pf)]
            send(h, c, "rl" + "+-"[d], 14 + d, piece, piece, dev)

    def gather2(h, c):
        copies[h, c, "rl+"].wait_recv()
        copies[h, c, "rl-"].wait_recv()
        pf, plus, minus = axes[h][0]
        mine = y.at[:, cols(h, c, pf)]
        send(h, c, "ag2+", 16, mine, mine, plus)
        send(h, c, "ag2-", 17, mine, mine, minus)

    def relay2(h, c):
        pf, plus, minus = axes[h][0]
        for d, dev in enumerate((plus, minus)):
            copies[h, c, "ag2" + "+-"[d]].wait_recv()
            seg = lax.rem(pf + 3 - 2 * d, side)
            piece = y.at[pl.ds(half * d, half), cols(h, c, seg)]
            send(h, c, "rl2" + "+-"[d], 18 + d, piece, piece, dev)

    def last(h, c):
        copies[h, c, "rl2+"].wait_recv()
        copies[h, c, "rl2-"].wait_recv()

    pl.semaphore_wait(barrier, 4)

    stages = (merge, second, merge2, gather, relay, gather2, relay2, last)
    for tick in range(chunks + len(stages)):
        if tick < chunks:
            for j in range(8 * tick, 8 * tick + 8):
                compute(j)
        for s in reversed(range(len(stages))):
            c = tick - s
            if 0 <= c < chunks:
                for h in range(2):
                    stages[s](h, c)

    for cp in copies.values():
        cp.wait_send()


def block(n, x, w_gate, w_up, w_down):
    rows, d = x.shape
    ff = w_gate.shape[1]
    side = 4
    assert n == side * side
    c = CHUNKS
    width = d // (2 * c * side)
    kchunk, nblock = min(KCHUNK, d), min(NBLOCK, ff)
    half, eighth = rows // 2, rows // 8
    vm = pltpu.VMEM
    dma = pltpu.SemaphoreType.DMA
    hbm = pl.BlockSpec(memory_space=pltpu.HBM)
    return pl.pallas_call(
        functools.partial(kernel, c, kchunk, nblock, DEPTH),
        out_shape=jax.ShapeDtypeStruct((rows, d), BF16),
        in_specs=[hbm] * 4,
        out_specs=pl.BlockSpec(memory_space=pltpu.VMEM),
        scratch_shapes=[
            vm((d // kchunk, rows, kchunk), BF16),
            vm((DEPTH, kchunk, nblock), BF16),
            vm((DEPTH, kchunk, nblock), BF16),
            vm((2 * c * side, ff, width), BF16),
            vm((rows, nblock), F32),
            vm((rows, nblock), F32),
            vm((rows, ff), BF16),
            vm((2, c, rows, width), F32),
            vm((2, c, 2, half, width), F32),
            vm((2, c, rows, width), BF16),
            vm((2, c, 2, half, width), BF16),
            vm((2, c, 2, half, width), BF16),
            vm((2, c, 2, half, width), BF16),
            vm((2, c, 2, half, width), BF16),
            vm((2, c, 2, half, width), BF16),
            vm((2, c, 2 * eighth, width), BF16),
            vm((2, c, 2, eighth, width), BF16),
            vm((2, c, 2, eighth, width), BF16),
            vm((2, c, 2, eighth, width), BF16),
            vm((2, c, 2, eighth, width), BF16),
            vm((2, c, 2, eighth, width), BF16),
            dma((d // kchunk,)),
            dma((DEPTH,)),
            dma((DEPTH,)),
            dma((2 * c * side,)),
            dma((2, c, 20)),
            dma((2, c, 20)),
        ],
        compiler_params=pltpu.CompilerParams(
            collective_id=0, has_side_effects=True, vmem_limit_bytes=48 * 2**20
        ),
        name="mlp",
    )(x, w_gate, w_up, w_down)


def solution(mesh):
    return jax.shard_map(
        functools.partial(block, mesh.shape["tp"]),
        mesh=mesh,
        in_specs=(P("dp", None), P(None, "tp"), P(None, "tp"), P("tp", None)),
        out_specs=P("dp", None),
        check_vma=False,
    )
```

time: 131 us -> 62.5 us (0.48)
  waiting for transfers between devices: 83.1 us -> 0 us
  Pallas kernels: 0 us -> 59.5 us
  matrix products: 29.7 us -> 0 us
  between operations: 13.4 us -> 0.01 us
  local copies, waits for them, and re-layouts: 4.68 us -> 2.91 us
    psum x1 -> x0, waiting for transfers between devices: 83.1 us -> none  [step(): return lax.psum(term, 'tp')]
    pallas_call x0 -> x1, Pallas kernels: none -> 59.5 us  [block(): pl.pallas_call(functools.partial(kernel, c, kchunk, nblock, DEPTH), out_s...]
    dot_general x2 -> x0, matrix products: 29.7 us -> none  [the longest x1 19.7 us: step(): jnp.dot(hidden, w_down, preferred_element_type=jnp.float32)]
    unnamed x3, local copies, waits for them, and re-layouts: 4.68 us -> 2.91 us
  transfers between devices with their start and end apart: 1 -> 0, of which waited for: 1 -> 0; matrix products, arithmetic and copies ran while one was open for 0% -> 0% of each run, Pallas kernels for 0% -> 0%
where the time goes in v1:
time: 62.5 us; the launch traced here: 62.4 us
  Pallas kernels  59.5 us (95%)
  local copies, waits for them, and re-layouts  2.91 us (5%)
    pallas_call x1, Pallas kernels, block(): pl.pallas_call(functools.partial(kernel, c, kchunk, nblock, DEPTH), out_s...  59.5 us
    unnamed x3, local copies, waits for them, and re-layouts  2.91 us

profile of v1, /device:TPU:96, one launch (start us, length us, event | category | flops | bytes accessed | tf_op | source)
XLA Modules:
  0.0 62.4 jit_solution(12683465887519805577)
XLA Ops:
  0.0 0.0 copy-start
  0.0 1.6 %copy-done = bf16[128,8192]{1,0:T(8,128)(2,1)S(1)} copy-done((bf16[128,8192]{1,0:T(8,128)(2,1)S(1)}, bf16[128,8192]{1,0:T(8,128)(2,1)}, u32[]{:S(2)}) %copy-start) | copy-done | bytes 2097176
  1.6 59.5 %mlp.1 = bf16[128,8192]{1,0:T(8,128)(2,1)S(1)} custom-call(bf16[128,8192]{1,0:T(8,128)(2,1)S(1)} %copy-done, bf16[8192,1536]{1,0:T(8,128)(2,1)} %wg_hbm.1, bf16[8192,1536]{1,0:T(8,128)(2,1)} %wu_hbm.1, bf16[1536,8192]{1,0:T(8,128)(2,1)} %wd_hbm.1), custom_call_target="tpu_custom_call" | custom-call | tf_op jit(solution)/shard_map/mlp/pallas_call | solution.py:254
  61.1 1.3 %copy.6 = bf16[128,8192]{1,0:T(8,128)(2,1)} copy(bf16[128,8192]{1,0:T(8,128)(2,1)S(1)} %mlp.1) | data formatting | bytes 4194304
Async XLA Ops:
  0.0 1.6 %copy-start = (bf16[128,8192]{1,0:T(8,128)(2,1)S(1)}, bf16[128,8192]{1,0:T(8,128)(2,1)}, u32[]{:S(2)}) copy-start(bf16[128,8192]{1,0:T(8,128)(2,1)} %x_hbm.1) | copy-start | bytes 6291460

commit v2 on v0

v2 whole, which is shorter than its diff:
```python
import functools

import jax
import jax.numpy as jnp
from jax import lax
from jax.experimental import pallas as pl
from jax.experimental.pallas import tpu as pltpu
from jax.sharding import PartitionSpec as P

MESH = pl.DeviceIdType.MESH
BF16, F32 = jnp.bfloat16, jnp.float32
GROUPS = ((2,), (2,), (2,), (2,))
NBLOCK = 512
KCHUNK = 1024
DEPTH = 4
AHEAD = 5
SCHEDULE = ("X0", "X1", "X2", "X3", "Y0", "M0", "Y1", "M1", "Y2", "M2", "Y3", "M3", "S0", "S1", "S2", "S3", "G0", "G1", "G2", "G3", "A0", "A1", "D2", "D3", "R0", "R1", "L0", "L1", "E2", "E3")


def kernel(
    groups, kchunk, nblock,
    x_hbm, wg_hbm, wu_hbm, wd_hbm, y,
    xv, gub, wdb, accg, accu, hid,
    xsem, gusem, wsem, ssem, rsem, *chunk_refs,
):
    widths = [w for group in groups for w in group]
    split = 4 * len(groups)
    own, tsum, qsum, tmrg = (chunk_refs[i:split:4] for i in range(4))
    keep, sstep, sdir, smrg, rstep, rboth = (chunk_refs[split + i :: 6] for i in range(6))
    where = [(g, sum(group[:i])) for g, group in enumerate(groups) for i in range(len(group))]
    gwidths = [sum(group) for group in groups]

    side = 4
    me = lax.axis_index("tp")
    px, py = me // side, lax.rem(me, side)

    def at(i, j):
        return lax.rem(i + side, side) * side + lax.rem(j + side, side)

    along = (
        (px, at(px + 1, py), at(px - 1, py), at(px + 2, py)),
        (py, at(px, py + 1), at(px, py - 1), at(px, py + 2)),
    )
    axes = (along, along[::-1])

    rows = xv.shape[1]
    ksteps = wg_hbm.shape[0] // kchunk
    nblocks = wg_hbm.shape[1] // nblock
    steps = ksteps * nblocks
    half, quarter, eighth = rows // 2, rows // 4, rows // 8
    ring = wdb.shape[0]

    def xcopy(k):
        return pltpu.make_async_copy(x_hbm.at[:, pl.ds(k * kchunk, kchunk)], xv.at[k], xsem.at[k])

    def gstart(i, slot):
        nb, k = i // ksteps, lax.rem(i, ksteps)
        src = (pl.ds(k * kchunk, kchunk), pl.ds(nb * nblock, nblock))
        pltpu.make_async_copy(wg_hbm.at[src], gub.at[slot, 0], gusem.at[slot]).start()
        pltpu.make_async_copy(wu_hbm.at[src], gub.at[slot, 1], gusem.at[slot]).start()

    def gwait(slot):
        pltpu.make_async_copy(gub.at[slot], gub.at[slot], gusem.at[slot]).wait()

    def cols(h, g, seg, skip=0, width=None):
        first = h * sum(widths) * side + sum(gwidths[:g]) * side + skip
        return pl.ds(pl.multiple_of(first + seg * gwidths[g], 128), width or gwidths[g])

    plan = SCHEDULE
    order = []
    for token in plan:
        order += [(int(token[1]), off) for off in {"X": (2,), "Y": (1, 3, 0)}.get(token[0], ())]

    def wstart(j):
        c, off = order[j]
        g, skip = where[c]
        for h in range(2):
            seg = lax.rem(axes[h][0][0] + off, side)
            pltpu.make_async_copy(
                wd_hbm.at[:, cols(h, g, seg, skip, widths[c])],
                wdb.at[j % ring, :, h * widths[c] : (h + 1) * widths[c]],
                wsem.at[j % ring],
            ).start()

    def wwait(j):
        buf = wdb.at[j % ring, :, : 2 * widths[order[j][0]]]
        pltpu.make_async_copy(buf, buf, wsem.at[j % ring]).wait()

    for i in range(DEPTH):
        xcopy(i).start()
        gstart(jnp.int32(i), i)
    for k in range(DEPTH, ksteps):
        xcopy(k).start()

    barrier = pltpu.get_barrier_semaphore()
    for _, *partners in along:
        for dev in partners:
            pl.semaphore_signal(barrier, inc=1, device_id={"tp": dev}, device_id_type=MESH)

    for nb in range(nblocks):
        accg[...] = jnp.zeros_like(accg)
        accu[...] = jnp.zeros_like(accu)

        @pl.loop(0, ksteps)
        def _(k, nb=nb):
            i = nb * ksteps + k
            slot = lax.rem(i, DEPTH)
            if nb == 0:
                xcopy(k).wait()
            gwait(slot)
            accg[...] += jnp.dot(xv[k], gub[slot, 0], preferred_element_type=F32)
            accu[...] += jnp.dot(xv[k], gub[slot, 1], preferred_element_type=F32)

            @pl.when(i + DEPTH < steps)
            def _():
                gstart(i + DEPTH, slot)

            if nb == nblocks - 1:
                for d in range(DEPTH):

                    @pl.when(i + DEPTH == steps + d)
                    def _(d=d):
                        for j in range(d * AHEAD // DEPTH, (d + 1) * AHEAD // DEPTH):
                            wstart(j)

        g = accg[...]
        hid[:, nb * nblock : (nb + 1) * nblock] = (jax.nn.silu(g) * accu[...]).astype(BF16)

    sent = []

    def send(sem, src, dst, dev):
        pltpu.make_async_remote_copy(
            src_ref=src, dst_ref=dst, send_sem=ssem, recv_sem=rsem.at[sem],
            device_id={"tp": dev}, device_id_type=MESH,
        ).start()
        sent.append(src.shape[0] * src.shape[1])

    def arrived(sem, like):
        pltpu.make_async_copy(like, like, rsem.at[sem]).wait()

    def gsem(g, stage):
        return 2 * len(widths) + 6 * g + stage

    def down(offs, c):
        for off in offs:
            j = order.index((c, off))
            if j + AHEAD < len(order):
                wstart(j + AHEAD)
            wwait(j)
            width = widths[c]
            g, skip = where[c]
            both = jnp.dot(hid[...], wdb[j % ring, :, : 2 * width], preferred_element_type=F32)
            for h in range(2):
                _, plus, minus, _ = axes[h][0]
                t = both[:, h * width : (h + 1) * width]
                if off == 2:
                    sstep[c][h] = t.astype(BF16)
                    send(2 * c, sstep[c].at[h, :half], rstep[c].at[h, 0], plus)
                    send(2 * c, sstep[c].at[h, half:], rstep[c].at[h, 1], minus)
                elif off == 1:
                    keep[c][h, 0] = t[:half]
                    sdir[c][h, 0] = t[half:].astype(BF16)
                    send(2 * c + 1, sdir[c].at[h, 0], rboth[c].at[h, 2], plus)
                elif off == 3:
                    keep[c][h, 1] = t[half:]
                    sdir[c][h, 1] = t[:half].astype(BF16)
                    send(2 * c + 1, sdir[c].at[h, 1], rboth[c].at[h, 3], minus)
                else:
                    own[g][h, :, skip : skip + width] = t

    def merge(c):
        arrived(2 * c, rstep[c])
        for h in range(2):
            _, plus, minus, _ = axes[h][0]
            for d, dev in enumerate((plus, minus)):
                smrg[c][h, d] = (keep[c][h, d] + rstep[c][h, d].astype(F32)).astype(BF16)
                send(2 * c + 1, smrg[c].at[h, d], rboth[c].at[h, d], dev)

    def sub(p, off):
        return pl.ds(pl.multiple_of(lax.rem(p + off, side) * quarter, quarter), quarter)

    def sub8(p, off, low):
        return pl.ds(pl.multiple_of(lax.rem(p + off, side) * quarter + low * eighth, eighth), eighth)

    def second(g):
        for c, (at_g, skip) in enumerate(where):
            if at_g != g:
                continue
            arrived(2 * c + 1, rboth[c])
            part = slice(skip, skip + widths[c])
            for h in range(2):
                top = own[g][h, :half, part] + (rboth[c][h, 0].astype(F32) + rboth[c][h, 3].astype(F32))
                low = own[g][h, half:, part] + (rboth[c][h, 1].astype(F32) + rboth[c][h, 2].astype(F32))
                own[g][h, :half, part] = top
                own[g][h, half:, part] = low
                tsum[g][h, :half, part] = top.astype(BF16)
                tsum[g][h, half:, part] = low.astype(BF16)
        for h in range(2):
            p, plus, minus, far = axes[h][1]
            if f"U{g}" in plan:
                for d, dev in enumerate((plus, minus)):
                    land = pl.ds(d * eighth, eighth)
                    send(gsem(g, 4), tsum[g].at[h, sub8(p, 2, d)], qsum[g].at[h, 0, land], dev)
                    send(gsem(g, 0), tsum[g].at[h, sub8(p, 1 + 2 * d, 1 - d)], qsum[g].at[h, 1, land], dev)
                continue
            for i, (off, dev) in enumerate(((2, far), (1, plus), (3, minus))):
                send(gsem(g, 0), tsum[g].at[h, sub(p, off)], qsum[g].at[h, i], dev)

    def merge2(g):
        arrived(gsem(g, 4), qsum[g].at[:, 0])
        for h in range(2):
            p, plus, minus, _ = axes[h][1]
            for d, dev in enumerate((plus, minus)):
                land = pl.ds(d * eighth, eighth)
                mine = own[g][h, sub8(p, 1 + 2 * d, d)]
                tmrg[g][h, d] = (mine + qsum[g][h, 0, land].astype(F32)).astype(BF16)
                send(gsem(g, 0), tmrg[g].at[h, d], qsum[g].at[h, 2, land], dev)

    def gather(g):
        merged = f"U{g}" in plan
        arrived(gsem(g, 0), qsum[g].at[:, 1:] if merged else qsum[g])
        for h in range(2):
            p, plus, minus, far = axes[h][1]
            pf = axes[h][0][0]
            if merged:
                for d in range(2):
                    total = own[g][h, sub8(p, 0, d)]
                    total += qsum[g][h, 2, d * eighth : (d + 1) * eighth].astype(F32)
                    total += qsum[g][h, 1, (1 - d) * eighth : (2 - d) * eighth].astype(F32)
                    y[sub8(p, 0, d), cols(h, g, pf)] = total.astype(BF16)
            else:
                total = own[g][h, sub(p, 0)]
                total += qsum[g][h, 0].astype(F32) + qsum[g][h, 1].astype(F32) + qsum[g][h, 2].astype(F32)
                y[sub(p, 0), cols(h, g, pf)] = total.astype(BF16)
            mine = y.at[sub(p, 0), cols(h, g, pf)]
            for dev in (plus, minus) if f"V{g}" in plan else (far, plus, minus):
                send(gsem(g, 1), mine, mine, dev)

    def relay1(g):
        arrived(gsem(g, 1), qsum[g].at[:, 1:])
        for h in range(2):
            p, plus, minus, _ = axes[h][1]
            for d, dev in enumerate((plus, minus)):
                piece = y.at[sub8(p, 3 - 2 * d, d), cols(h, g, axes[h][0][0])]
                send(gsem(g, 5), piece, piece, dev)

    def gather2(g, direct=False):
        if f"V{g}" in plan:
            arrived(gsem(g, 5), qsum[g].at[:, 0])
        else:
            arrived(gsem(g, 1), qsum[g])
        for h in range(2):
            pf, plus, minus, far = axes[h][0]
            mine = y.at[:, cols(h, g, pf)]
            if direct:
                send(gsem(g, 3), mine, mine, far)
            for dev in (plus, minus):
                send(gsem(g, 2), mine, mine, dev)

    def relay(g):
        arrived(gsem(g, 2), y.at[:, : 4 * gwidths[g]])
        for h in range(2):
            pf, plus, minus, _ = axes[h][0]
            for d, dev in enumerate((plus, minus)):
                seg = lax.rem(pf + 3 - 2 * d, side)
                piece = y.at[pl.ds(half * d, half), cols(h, g, seg)]
                send(gsem(g, 3), piece, piece, dev)

    def last(g, direct=False):
        if direct:
            arrived(gsem(g, 2), y.at[:, : 4 * gwidths[g]])
        arrived(gsem(g, 3), y.at[:, : 2 * gwidths[g]])

    pl.semaphore_wait(barrier, 6)

    stages = {
        "X": functools.partial(down, (2,)), "Y": functools.partial(down, (1, 3, 0)),
        "M": merge, "S": second, "U": merge2, "V": relay1, "G": gather, "A": gather2, "R": relay, "L": last,
        "D": functools.partial(gather2, direct=True), "E": functools.partial(last, direct=True),
    }
    for token in plan:
        stages[token[0]](int(token[1]))

    wait_rows = sum(sent) // nblock
    flat = gub.reshape(-1, nblock)
    pltpu.make_async_copy(flat.at[:wait_rows], flat.at[:wait_rows], ssem).wait()


def block(n, x, w_gate, w_up, w_down):
    rows, d = x.shape
    ff = w_gate.shape[1]
    side = 4
    assert n == side * side
    unit = d // (2 * side * sum(sum(group) for group in GROUPS))
    groups = tuple(tuple(w * unit for w in group) for group in GROUPS)
    widths = [w for group in groups for w in group]
    kchunk, nblock = min(KCHUNK, d), min(NBLOCK, ff)
    half = rows // 2
    vm = pltpu.VMEM
    dma = pltpu.SemaphoreType.DMA
    chunk_scratch = []
    for w in map(sum, groups):
        chunk_scratch += [
            vm((2, rows, w), F32),
            vm((2, rows, w), BF16),
            vm((2, 3, rows // 4, w), BF16),
            vm((2, 2, rows // 8, w), BF16),
        ]
    for w in widths:
        chunk_scratch += [
            vm((2, 2, half, w), F32),
            vm((2, rows, w), BF16),
            vm((2, 2, half, w), BF16),
            vm((2, 2, half, w), BF16),
            vm((2, 2, half, w), BF16),
            vm((2, 4, half, w), BF16),
        ]
    hbm = pl.BlockSpec(memory_space=pltpu.HBM)
    return pl.pallas_call(
        functools.partial(kernel, groups, kchunk, nblock),
        out_shape=jax.ShapeDtypeStruct((rows, d), BF16),
        in_specs=[hbm] * 4,
        out_specs=pl.BlockSpec(memory_space=pltpu.VMEM),
        scratch_shapes=[
            vm((d // kchunk, rows, kchunk), BF16),
            vm((DEPTH, 2, kchunk, nblock), BF16),
            vm((AHEAD + 1, ff, 2 * max(widths)), BF16),
            vm((rows, nblock), F32),
            vm((rows, nblock), F32),
            vm((rows, ff), BF16),
            dma((d // kchunk,)),
            dma((DEPTH,)),
            dma((AHEAD + 1,)),
            dma(()),
            dma((2 * len(widths) + 6 * len(groups),)),
            *chunk_scratch,
        ],
        compiler_params=pltpu.CompilerParams(
            collective_id=0, has_side_effects=True, vmem_limit_bytes=50 * 2**20
        ),
        name="mlp",
    )(x, w_gate, w_up, w_down)


def solution(mesh):
    return jax.shard_map(
        functools.partial(block, mesh.shape["tp"]),
        mesh=mesh,
        in_specs=(P("dp", None), P(None, "tp"), P(None, "tp"), P("tp", None)),
        out_specs=P("dp", None),
        check_vma=False,
    )
```

time: 131 us -> 51.1 us (0.39)
  waiting for transfers between devices: 83.1 us -> 0 us
  Pallas kernels: 0 us -> 49.7 us
  matrix products: 29.7 us -> 0 us
  between operations: 13.4 us -> 0.01 us
  local copies, waits for them, and re-layouts: 4.68 us -> 1.32 us
    psum x1 -> x0, waiting for transfers between devices: 83.1 us -> none  [step(): return lax.psum(term, 'tp')]
    pallas_call x0 -> x1, Pallas kernels: none -> 49.7 us  [block(): pl.pallas_call(functools.partial(kernel, groups, kchunk, nblock), out_sha...]
    dot_general x2 -> x0, matrix products: 29.7 us -> none  [the longest x1 19.7 us: step(): jnp.dot(hidden, w_down, preferred_element_type=jnp.float32)]
    unnamed x3 -> x1, local copies, waits for them, and re-layouts: 4.68 us -> 1.32 us
  transfers between devices with their start and end apart: 1 -> 0, of which waited for: 1 -> 0; matrix products, arithmetic and copies ran while one was open for 0% -> 0% of each run, Pallas kernels for 0% -> 0%
where the time goes in v2:
time: 51.1 us; the launch traced here: 51 us
  Pallas kernels  49.7 us (97%)
  local copies, waits for them, and re-layouts  1.32 us (3%)
    pallas_call x1, Pallas kernels, block(): pl.pallas_call(functools.partial(kernel, groups, kchunk, nblock), out_sha...  49.7 us
    unnamed x1, local copies, waits for them, and re-layouts  1.32 us

profile of v2, /device:TPU:96, one launch (start us, length us, event | category | flops | bytes accessed | tf_op | source)
XLA Modules:
  0.0 51.0 jit_solution(16846405195195399886)
XLA Ops:
  0.0 49.7 %mlp.1 = bf16[128,8192]{1,0:T(8,128)(2,1)S(1)} custom-call(bf16[128,8192]{1,0:T(8,128)(2,1)} %x_hbm.1, bf16[8192,1536]{1,0:T(8,128)(2,1)} %wg_hbm.1, bf16[8192,1536]{1,0:T(8,128)(2,1)} %wu_hbm.1, bf16[1536,8192]{1,0:T(8,128)(2,1)} %wd_hbm.1), custom_call_target="tpu_custom_call" | custom-call | tf_op jit(solution)/shard_map/mlp/pallas_call | solution.py:319
  49.7 1.3 %copy.6 = bf16[128,8192]{1,0:T(8,128)(2,1)} copy(bf16[128,8192]{1,0:T(8,128)(2,1)S(1)} %mlp.1) | data formatting | bytes 4194304

commit v3 on v2

--- a/solution.py
+++ b/solution.py
@@ -14,7 +14,7 @@
 KCHUNK = 1024
 DEPTH = 4
 AHEAD = 5
-SCHEDULE = ("X0", "X1", "X2", "X3", "Y0", "M0", "Y1", "M1", "Y2", "M2", "Y3", "M3", "S0", "S1", "S2", "S3", "G0", "G1", "G2", "G3", "A0", "A1", "D2", "D3", "R0", "R1", "L0", "L1", "E2", "E3")
+SCHEDULE = ('X0', 'X1', 'X2', 'X3', 'Y0', 'M0', 'Y1', 'M1', 'Y2', 'M2', 'Y3', 'M3', 'S0', 'S1', 'S2', 'S3', 'G0', 'G1', 'G2', 'G3', 'A0', 'A1', 'D2', 'D3', 'R0', 'R1', 'L0', 'L1', 'E2', 'E3')
 
 
 def kernel(
@@ -235,6 +235,21 @@
             mine = y.at[sub(p, 0), cols(h, g, pf)]
             for dev in (plus, minus) if f"V{g}" in plan else (far, plus, minus):
                 send(gsem(g, 1), mine, mine, dev)
+        for h in range(2):
+            along_first(h, g, ((0, 0), (1, 0)))
+
+    def along_first(h, g, pieces):
+        p = axes[h][1][0]
+        pf, plus, minus, far = axes[h][0]
+        for d, off in pieces:
+            piece = y.at[sub(p, off), cols(h, g, pf)]
+            if f"D{g}" in plan:
+                send(gsem(g, 2), piece, piece, (plus, minus)[d])
+                if d == 0:
+                    send(gsem(g, 3), piece, piece, far)
+            else:
+                relayed = (off < 2) == (d == 0)
+                send(gsem(g, 2 if relayed else 3), piece, piece, (plus, minus)[d])
 
     def relay1(g):
         arrived(gsem(g, 1), qsum[g].at[:, 1:])
@@ -244,39 +259,36 @@
                 piece = y.at[sub8(p, 3 - 2 * d, d), cols(h, g, axes[h][0][0])]
                 send(gsem(g, 5), piece, piece, dev)
 
-    def gather2(g, direct=False):
+    def gather2(g):
         if f"V{g}" in plan:
             arrived(gsem(g, 5), qsum[g].at[:, 0])
         else:
             arrived(gsem(g, 1), qsum[g])
         for h in range(2):
-            pf, plus, minus, far = axes[h][0]
-            mine = y.at[:, cols(h, g, pf)]
-            if direct:
-                send(gsem(g, 3), mine, mine, far)
-            for dev in (plus, minus):
-                send(gsem(g, 2), mine, mine, dev)
+            along_first(h, g, ((0, 1), (1, 2), (1, 3), (1, 1), (0, 2), (0, 3)))
 
     def relay(g):
-        arrived(gsem(g, 2), y.at[:, : 4 * gwidths[g]])
-        for h in range(2):
+        arrived(gsem(g, 2), y.at[:, : 2 * gwidths[g]])
+        for h in range(2):
+            p = axes[h][1][0]
             pf, plus, minus, _ = axes[h][0]
             for d, dev in enumerate((plus, minus)):
                 seg = lax.rem(pf + 3 - 2 * d, side)
-                piece = y.at[pl.ds(half * d, half), cols(h, g, seg)]
-                send(gsem(g, 3), piece, piece, dev)
+                for off in (2 * d, 2 * d + 1):
+                    piece = y.at[sub(p, off), cols(h, g, seg)]
+                    send(gsem(g, 3), piece, piece, dev)
 
     def last(g, direct=False):
         if direct:
             arrived(gsem(g, 2), y.at[:, : 4 * gwidths[g]])
-        arrived(gsem(g, 3), y.at[:, : 2 * gwidths[g]])
+        arrived(gsem(g, 3), y.at[:, : (2 if direct else 4) * gwidths[g]])
 
     pl.semaphore_wait(barrier, 6)
 
     stages = {
         "X": functools.partial(down, (2,)), "Y": functools.partial(down, (1, 3, 0)),
         "M": merge, "S": second, "U": merge2, "V": relay1, "G": gather, "A": gather2, "R": relay, "L": last,
-        "D": functools.partial(gather2, direct=True), "E": functools.partial(last, direct=True),
+        "D": gather2, "E": functools.partial(last, direct=True),
     }
     for token in plan:
         stages[token[0]](int(token[1]))

time: 51.1 us -> 50.3 us (0.984)
  Pallas kernels: 49.7 us -> 48.9 us
    pallas_call x1, Pallas kernels: 49.7 us -> 48.9 us  [block(): pl.pallas_call(functools.partial(kernel, groups, kchunk, nblock), out_sha...]
where the time goes in v3:
time: 50.3 us; the launch traced here: 50.2 us
  Pallas kernels  48.9 us (97%)
  local copies, waits for them, and re-layouts  1.32 us (3%)
    pallas_call x1, Pallas kernels, block(): pl.pallas_call(functools.partial(kernel, groups, kchunk, nblock), out_sha...  48.9 us
    unnamed x1, local copies, waits for them, and re-layouts  1.32 us

profile of v3, /device:TPU:96, one launch (start us, length us, event | category | flops | bytes accessed | tf_op | source)
XLA Modules:
  0.0 50.2 jit_solution(15605726606671851612)
XLA Ops:
  0.0 48.9 %mlp.1 = bf16[128,8192]{1,0:T(8,128)(2,1)S(1)} custom-call(bf16[128,8192]{1,0:T(8,128)(2,1)} %x_hbm.1, bf16[8192,1536]{1,0:T(8,128)(2,1)} %wg_hbm.1, bf16[8192,1536]{1,0:T(8,128)(2,1)} %wu_hbm.1, bf16[1536,8192]{1,0:T(8,128)(2,1)} %wd_hbm.1), custom_call_target="tpu_custom_call" | custom-call | tf_op jit(solution)/shard_map/mlp/pallas_call | solution.py:331
  48.9 1.3 %copy.6 = bf16[128,8192]{1,0:T(8,128)(2,1)} copy(bf16[128,8192]{1,0:T(8,128)(2,1)S(1)} %mlp.1) | data formatting | bytes 4194304

commit v4 on v3

--- a/solution.py
+++ b/solution.py
@@ -10,11 +10,11 @@
 MESH = pl.DeviceIdType.MESH
 BF16, F32 = jnp.bfloat16, jnp.float32
 GROUPS = ((2,), (2,), (2,), (2,))
-NBLOCK = 512
+NBLOCK = 768
 KCHUNK = 1024
 DEPTH = 4
 AHEAD = 5
-SCHEDULE = ('X0', 'X1', 'X2', 'X3', 'Y0', 'M0', 'Y1', 'M1', 'Y2', 'M2', 'Y3', 'M3', 'S0', 'S1', 'S2', 'S3', 'G0', 'G1', 'G2', 'G3', 'A0', 'A1', 'D2', 'D3', 'R0', 'R1', 'L0', 'L1', 'E2', 'E3')
+SCHEDULE = ('X0', 'X1', 'X2', 'X3', 'Y0', 'M0', 'Y1', 'M1', 'Y2', 'M2', 'Y3', 'M3', 'S0', 'S1', 'S2', 'S3', 'G0', 'G1', 'G2', 'G3', 'A0', 'A1', 'D2', 'D3', 'R0', 'R1')
 
 
 def kernel(
@@ -24,8 +24,8 @@
     xsem, gusem, wsem, ssem, rsem, *chunk_refs,
 ):
     widths = [w for group in groups for w in group]
-    split = 4 * len(groups)
-    own, tsum, qsum, tmrg = (chunk_refs[i:split:4] for i in range(4))
+    split = 3 * len(groups)
+    own, tsum, qsum = (chunk_refs[i:split:3] for i in range(3))
     keep, sstep, sdir, smrg, rstep, rboth = (chunk_refs[split + i :: 6] for i in range(6))
     where = [(g, sum(group[:i])) for g, group in enumerate(groups) for i in range(len(group))]
     gwidths = [sum(group) for group in groups]
@@ -47,7 +47,7 @@
     ksteps = wg_hbm.shape[0] // kchunk
     nblocks = wg_hbm.shape[1] // nblock
     steps = ksteps * nblocks
-    half, quarter, eighth = rows // 2, rows // 4, rows // 8
+    half, quarter = rows // 2, rows // 4
     ring = wdb.shape[0]
 
     def xcopy(k):
@@ -139,7 +139,7 @@
         pltpu.make_async_copy(like, like, rsem.at[sem]).wait()
 
     def gsem(g, stage):
-        return 2 * len(widths) + 6 * g + stage
+        return 2 * len(widths) + (0 if stage == 3 else 1 + 3 * g + stage)
 
     def down(offs, c):
         for off in offs:
@@ -179,9 +179,6 @@
     def sub(p, off):
         return pl.ds(pl.multiple_of(lax.rem(p + off, side) * quarter, quarter), quarter)
 
-    def sub8(p, off, low):
-        return pl.ds(pl.multiple_of(lax.rem(p + off, side) * quarter + low * eighth, eighth), eighth)
-
     def second(g):
         for c, (at_g, skip) in enumerate(where):
             if at_g != g:
@@ -197,43 +194,19 @@
                 tsum[g][h, half:, part] = low.astype(BF16)
         for h in range(2):
             p, plus, minus, far = axes[h][1]
-            if f"U{g}" in plan:
-                for d, dev in enumerate((plus, minus)):
-                    land = pl.ds(d * eighth, eighth)
-                    send(gsem(g, 4), tsum[g].at[h, sub8(p, 2, d)], qsum[g].at[h, 0, land], dev)
-                    send(gsem(g, 0), tsum[g].at[h, sub8(p, 1 + 2 * d, 1 - d)], qsum[g].at[h, 1, land], dev)
-                continue
             for i, (off, dev) in enumerate(((2, far), (1, plus), (3, minus))):
                 send(gsem(g, 0), tsum[g].at[h, sub(p, off)], qsum[g].at[h, i], dev)
 
-    def merge2(g):
-        arrived(gsem(g, 4), qsum[g].at[:, 0])
-        for h in range(2):
-            p, plus, minus, _ = axes[h][1]
-            for d, dev in enumerate((plus, minus)):
-                land = pl.ds(d * eighth, eighth)
-                mine = own[g][h, sub8(p, 1 + 2 * d, d)]
-                tmrg[g][h, d] = (mine + qsum[g][h, 0, land].astype(F32)).astype(BF16)
-                send(gsem(g, 0), tmrg[g].at[h, d], qsum[g].at[h, 2, land], dev)
-
     def gather(g):
-        merged = f"U{g}" in plan
-        arrived(gsem(g, 0), qsum[g].at[:, 1:] if merged else qsum[g])
+        arrived(gsem(g, 0), qsum[g])
         for h in range(2):
             p, plus, minus, far = axes[h][1]
             pf = axes[h][0][0]
-            if merged:
-                for d in range(2):
-                    total = own[g][h, sub8(p, 0, d)]
-                    total += qsum[g][h, 2, d * eighth : (d + 1) * eighth].astype(F32)
-                    total += qsum[g][h, 1, (1 - d) * eighth : (2 - d) * eighth].astype(F32)
-                    y[sub8(p, 0, d), cols(h, g, pf)] = total.astype(BF16)
-            else:
-                total = own[g][h, sub(p, 0)]
-                total += qsum[g][h, 0].astype(F32) + qsum[g][h, 1].astype(F32) + qsum[g][h, 2].astype(F32)
-                y[sub(p, 0), cols(h, g, pf)] = total.astype(BF16)
+            total = own[g][h, sub(p, 0)]
+            total += qsum[g][h, 0].astype(F32) + qsum[g][h, 1].astype(F32) + qsum[g][h, 2].astype(F32)
+            y[sub(p, 0), cols(h, g, pf)] = total.astype(BF16)
             mine = y.at[sub(p, 0), cols(h, g, pf)]
-            for dev in (plus, minus) if f"V{g}" in plan else (far, plus, minus):
+            for dev in (far, plus, minus):
                 send(gsem(g, 1), mine, mine, dev)
         for h in range(2):
             along_first(h, g, ((0, 0), (1, 0)))
@@ -251,19 +224,8 @@
                 relayed = (off < 2) == (d == 0)
                 send(gsem(g, 2 if relayed else 3), piece, piece, (plus, minus)[d])
 
-    def relay1(g):
-        arrived(gsem(g, 1), qsum[g].at[:, 1:])
-        for h in range(2):
-            p, plus, minus, _ = axes[h][1]
-            for d, dev in enumerate((plus, minus)):
-                piece = y.at[sub8(p, 3 - 2 * d, d), cols(h, g, axes[h][0][0])]
-                send(gsem(g, 5), piece, piece, dev)
-
     def gather2(g):
-        if f"V{g}" in plan:
-            arrived(gsem(g, 5), qsum[g].at[:, 0])
-        else:
-            arrived(gsem(g, 1), qsum[g])
+        arrived(gsem(g, 1), qsum[g])
         for h in range(2):
             along_first(h, g, ((0, 1), (1, 2), (1, 3), (1, 1), (0, 2), (0, 3)))
 
@@ -278,22 +240,24 @@
                     piece = y.at[sub(p, off), cols(h, g, seg)]
                     send(gsem(g, 3), piece, piece, dev)
 
-    def last(g, direct=False):
-        if direct:
-            arrived(gsem(g, 2), y.at[:, : 4 * gwidths[g]])
-        arrived(gsem(g, 3), y.at[:, : (2 if direct else 4) * gwidths[g]])
-
     pl.semaphore_wait(barrier, 6)
 
     stages = {
         "X": functools.partial(down, (2,)), "Y": functools.partial(down, (1, 3, 0)),
-        "M": merge, "S": second, "U": merge2, "V": relay1, "G": gather, "A": gather2, "R": relay, "L": last,
-        "D": gather2, "E": functools.partial(last, direct=True),
+        "M": merge, "S": second, "G": gather, "A": gather2, "R": relay, "D": gather2,
     }
     for token in plan:
         stages[token[0]](int(token[1]))
 
+    total = 0
+    for g, w in enumerate(gwidths):
+        if f"D{g}" in plan:
+            arrived(gsem(g, 2), y.at[:, : 4 * w])
+        total += (2 if f"D{g}" in plan else 4) * w
+    arrived(gsem(0, 3), y.at[:, :total])
+
     wait_rows = sum(sent) // nblock
+    assert wait_rows * nblock == sum(sent)
     flat = gub.reshape(-1, nblock)
     pltpu.make_async_copy(flat.at[:wait_rows], flat.at[:wait_rows], ssem).wait()
 
@@ -316,7 +280,6 @@
             vm((2, rows, w), F32),
             vm((2, rows, w), BF16),
             vm((2, 3, rows // 4, w), BF16),
-            vm((2, 2, rows // 8, w), BF16),
         ]
     for w in widths:
         chunk_scratch += [
@@ -344,7 +307,7 @@
             dma((DEPTH,)),
             dma((AHEAD + 1,)),
             dma(()),
-            dma((2 * len(widths) + 6 * len(groups),)),
+            dma((2 * len(widths) + 1 + 3 * len(groups),)),
             *chunk_scratch,
         ],
         compiler_params=pltpu.CompilerParams(

time: 50.3 us -> 49.9 us (level)
  no operation moved by 1% of the time
where the time goes in v4:
time: 49.9 us
  Pallas kernels  48.5 us (97%)
  local copies, waits for them, and re-layouts  1.32 us (3%)
    pallas_call x1, Pallas kernels, block(): pl.pallas_call(functools.partial(kernel, groups, kchunk, nblock), out_sha...  48.5 us
    unnamed x1, local copies, waits for them, and re-layouts  1.32 us

profile of v4, /device:TPU:96, one launch (start us, length us, event | category | flops | bytes accessed | tf_op | source)
XLA Modules:
  0.0 49.9 jit_solution(17092800380218790697)
XLA Ops:
  0.0 48.5 %mlp.1 = bf16[128,8192]{1,0:T(8,128)(2,1)S(1)} custom-call(bf16[128,8192]{1,0:T(8,128)(2,1)} %x_hbm.1, bf16[8192,1536]{1,0:T(8,128)(2,1)} %wg_hbm.1, bf16[8192,1536]{1,0:T(8,128)(2,1)} %wu_hbm.1, bf16[1536,8192]{1,0:T(8,128)(2,1)} %wd_hbm.1), custom_call_target="tpu_custom_call" | custom-call | tf_op jit(solution)/shard_map/mlp/pallas_call | solution.py:294
  48.5 1.3 %copy.6 = bf16[128,8192]{1,0:T(8,128)(2,1)} copy(bf16[128,8192]{1,0:T(8,128)(2,1)S(1)} %mlp.1) | data formatting | bytes 4194304

commit v5 on v4

--- a/solution.py
+++ b/solution.py
@@ -9,12 +9,12 @@
 
 MESH = pl.DeviceIdType.MESH
 BF16, F32 = jnp.bfloat16, jnp.float32
-GROUPS = ((2,), (2,), (2,), (2,))
+GROUPS = ((2,), (2,), (2,), (1,), (1,))
 NBLOCK = 768
 KCHUNK = 1024
 DEPTH = 4
 AHEAD = 5
-SCHEDULE = ('X0', 'X1', 'X2', 'X3', 'Y0', 'M0', 'Y1', 'M1', 'Y2', 'M2', 'Y3', 'M3', 'S0', 'S1', 'S2', 'S3', 'G0', 'G1', 'G2', 'G3', 'A0', 'A1', 'D2', 'D3', 'R0', 'R1')
+SCHEDULE = ('X0', 'X1', 'X2', 'X3', 'X4', 'Y0', 'M0', 'Y1', 'M1', 'Y2', 'M2', 'Y3', 'M3', 'Y4', 'M4', 'S0', 'S1', 'S2', 'S3', 'S4', 'G0', 'G1', 'G2', 'G3', 'G4', 'A0', 'A1', 'A2', 'D3', 'D4', 'R0', 'R1', 'R2')
 
 
 def kernel(

time: 49.9 us -> 49.6 us (level)
  no operation moved by 1% of the time
where the time goes in v5:
time: 49.6 us
  Pallas kernels  48.2 us (97%)
  local copies, waits for them, and re-layouts  1.32 us (3%)
    pallas_call x1, Pallas kernels, block(): pl.pallas_call(functools.partial(kernel, groups, kchunk, nblock), out_sha...  48.2 us
    unnamed x1, local copies, waits for them, and re-layouts  1.32 us

profile of v5, /device:TPU:96, one launch (start us, length us, event | category | flops | bytes accessed | tf_op | source)
XLA Modules:
  0.0 49.6 jit_solution(8791863846599626354)
XLA Ops:
  0.0 48.2 %mlp.1 = bf16[128,8192]{1,0:T(8,128)(2,1)S(1)} custom-call(bf16[128,8192]{1,0:T(8,128)(2,1)} %x_hbm.1, bf16[8192,1536]{1,0:T(8,128)(2,1)} %wg_hbm.1, bf16[8192,1536]{1,0:T(8,128)(2,1)} %wu_hbm.1, bf16[1536,8192]{1,0:T(8,128)(2,1)} %wd_hbm.1), custom_call_target="tpu_custom_call" | custom-call | tf_op jit(solution)/shard_map/mlp/pallas_call | solution.py:294
  48.2 1.3 %copy.6 = bf16[128,8192]{1,0:T(8,128)(2,1)} copy(bf16[128,8192]{1,0:T(8,128)(2,1)S(1)} %mlp.1) | data formatting | bytes 4194304
